TPU v7x, 32 devices: a whole 2x2x4 slice. The times are simulated.
32 devices in a mesh: grp: 2 (over y), seq: 4 (over z), head: 2 (over x), batch: 2 (over core).
Axes of the slice: x: 2, y: 2, z: 4, core: 2. Of those that a mesh axis runs over, the one named last changes fastest.
Arguments:
- queries: bfloat16 [64, 64, 128], P(('grp', 'batch'), 'head'), parts along dimension 0, may hold values from -8 to 8
- key_cache: bfloat16 [64, 8, 1024, 128], P(('grp', 'batch'), 'head', 'seq'), parts along dimension 0, may hold values from -5 to 5
- value_cache: bfloat16 [64, 8, 1024, 128], P(('grp', 'batch'), 'head', 'seq'), parts along dimension 0, may hold values from -5 to 5
- gate_logits: float32 [2, 64, 64], P(None, ('grp', 'batch'), 'head'), parts along dimension 1, may hold values from -6 to 6
- lengths: int32 [64], P(('grp', 'batch')), parts along dimension 0, may hold values from 256 to 1024, as said below
- chosen: int32 [64, 8, 2], P(('grp', 'batch'), 'head'), parts along dimension 0, may hold values from 0 to 7, as said below
- counts: int32 [64, 8], P(('grp', 'batch'), 'head'), parts along dimension 0, may hold values from 1 to 2, as said below
Outputs:
- output: bfloat16 [64, 64, 128], P(('grp', 'batch'), 'head'), parts along dimension 0
There are 2 independent parts, one for each index of `grp`. A program takes and returns all parts, laid end to end along the dimension named above; each array names one. Nothing has to cross between parts.
Inputs may be any that keep to these rules, and one draw needn't show every extreme that they name: `lengths`: every draw has a sequence of the full length 1024. `chosen`: for each sequence and key-value head the first counts entries are distinct blocks that start below the sequence's length, and the first entry is block 0; the entries after them are ignored. `counts`: every draw has a sequence with 2 valid entries for every key-value head.
All inputs are finite; a program needn't handle non-finite values.
Results may differ from a plain program's by a relative error of at most 0.02.
Values may be sent and summed in bfloat16 or wider, within the bound.
A program may use at most 64 MiB of HBM per device.

v0:
```python
import math
import jax
import jax.numpy as jnp
from jax import lax
from jax.sharding import PartitionSpec as P

BLOCK = 128


def combined_all(array, axis, join):
    gathered = jax.tree.map(
        lambda a, kind: lax.all_gather(a.astype(kind), axis),
        array,
        (jnp.bfloat16, jnp.bfloat16, jnp.bfloat16),
    )

    def take(source):
        return jax.tree.map(
            lambda a, own: lax.dynamic_index_in_dim(a, source, 0, False).astype(own.dtype),
            gathered,
            array,
        )

    return lax.fori_loop(
        1, lax.axis_size(axis), lambda source, state: join(state, take(source)), take(0)
    )


def softmax_terms(query_rows, key_rows, value_rows, live_mask, score_scale):
    scores = (
        jnp.einsum("pgd,pnd->pgn", query_rows, key_rows, preferred_element_type=jnp.float32)
        * score_scale
    )
    scores = jnp.where(live_mask[:, None, :], scores, -1e30)
    row_max = jnp.max(scores, axis=2)
    weights = jnp.where(live_mask[:, None, :], jnp.exp(scores - row_max[:, :, None]), 0.0)
    weight_sum = jnp.sum(weights, axis=2)
    summed = jnp.einsum(
        "pgn,pnd->pgd", weights.astype(jnp.bfloat16), value_rows, preferred_element_type=jnp.float32
    )
    return (row_max, weight_sum, summed)


def combine(first, second):
    merged = []
    for index in range(0, len(first), 3):
        row_max = jnp.maximum(first[index], second[index])
        factor_first = jnp.exp(first[index] - row_max)
        factor_second = jnp.exp(second[index] - row_max)
        merged.append(row_max)
        merged.append(first[index + 1] * factor_first + second[index + 1] * factor_second)
        merged.append(
            first[index + 2] * factor_first[:, :, None]
            + second[index + 2] * factor_second[:, :, None]
        )
    return tuple(merged)


def finish(weight_sum, summed):
    return summed / weight_sum[:, :, None]


def pool_blocks(key_rows, value_rows, pair_lengths, first_block):
    pair_count, tokens, head_width = key_rows.shape
    block_count = tokens // BLOCK
    position = first_block * BLOCK + jnp.arange(tokens, dtype=jnp.int32)
    live_mask = position[None, :] < pair_lengths[:, None]
    token_ones = live_mask.astype(jnp.bfloat16).reshape(pair_count, block_count, BLOCK)
    starts = (first_block + jnp.arange(block_count, dtype=jnp.int32)) * BLOCK
    filled = jnp.clip(pair_lengths[:, None] - starts[None, :], 0, BLOCK)
    root_fill = jnp.sqrt(jnp.maximum(filled, 1).astype(jnp.float32))[:, :, None]
    key_sums = jnp.einsum(
        "pjt,pjtd->pjd",
        token_ones,
        key_rows.reshape(pair_count, block_count, BLOCK, head_width),
        preferred_element_type=jnp.float32,
    )
    value_sums = jnp.einsum(
        "pjt,pjtd->pjd",
        token_ones,
        value_rows.reshape(pair_count, block_count, BLOCK, head_width),
        preferred_element_type=jnp.float32,
    )
    pooled_keys = (key_sums / root_fill).astype(jnp.bfloat16)
    pooled_values = (value_sums / root_fill).astype(jnp.bfloat16)
    return (live_mask, filled > 0, pooled_keys, pooled_values)


def picked_tokens(live_mask, chosen_rows, count_rows, first_block):
    pair_count, tokens = live_mask.shape
    block_count = tokens // BLOCK
    block_ids = first_block + jnp.arange(block_count, dtype=jnp.int32)
    slot_live = jnp.arange(chosen_rows.shape[1], dtype=jnp.int32)[None, :] < count_rows[:, None]
    picked = jnp.any(
        (chosen_rows[:, :, None] == block_ids[None, None, :]) & slot_live[:, :, None], axis=1
    )
    spread = jnp.broadcast_to(picked[:, :, None], (pair_count, block_count, BLOCK)).reshape(
        pair_count, tokens
    )
    return live_mask & spread


def blend_gates(compressed, selected, gate_pairs):
    mixed = gate_pairs[0][:, :, None] * compressed + gate_pairs[1][:, :, None] * selected
    return mixed.astype(jnp.bfloat16)


def on_device(queries, key_cache, value_cache, gate_logits, lengths, chosen, counts):
    batch_rows, head_count, context, head_width = key_cache.shape
    pair_count = batch_rows * head_count
    group_size = queries.shape[1] // head_count
    score_scale = 1.0 / math.sqrt(head_width)
    query_rows = queries.reshape(pair_count, group_size, head_width)
    pair_keys = key_cache.reshape(pair_count, context, head_width)
    pair_values = value_cache.reshape(pair_count, context, head_width)
    pair_lengths = jnp.broadcast_to(lengths[:, None], (batch_rows, head_count)).reshape(pair_count)
    pair_chosen = chosen.reshape(pair_count, chosen.shape[2])
    pair_counts = counts.reshape(pair_count)
    gate_pairs = jax.nn.sigmoid(gate_logits.reshape(2, pair_count, group_size))
    local_blocks = context // BLOCK
    first_block = lax.axis_index("seq") * local_blocks
    live_mask, block_live, pooled_keys, pooled_values = pool_blocks(
        pair_keys, pair_values, pair_lengths, first_block
    )
    token_mask = picked_tokens(live_mask, pair_chosen, pair_counts, first_block)
    all_keys, all_values = (
        lax.all_gather(pooled_keys, "seq", axis=1, tiled=True),
        lax.all_gather(pooled_values, "seq", axis=1, tiled=True),
    )
    all_starts = jnp.arange(all_keys.shape[1], dtype=jnp.int32) * BLOCK
    all_live = all_starts[None, :] < pair_lengths[:, None]
    s_max, s_sum, s_val = softmax_terms(query_rows, pair_keys, pair_values, token_mask, score_scale)
    merged = combined_all((s_max, s_sum, s_val), "seq", combine)
    c_max, c_sum, c_val = softmax_terms(query_rows, all_keys, all_values, all_live, score_scale)
    output = blend_gates(finish(c_sum, c_val), finish(merged[1], merged[2]), gate_pairs)
    return output.reshape(batch_rows, head_count * group_size, head_width)


def solution(mesh):
    return jax.shard_map(
        on_device,
        mesh=mesh,
        in_specs=(
            P(("grp", "batch"), "head", None),
            P(("grp", "batch"), "head", "seq", None),
            P(("grp", "batch"), "head", "seq", None),
            P(None, ("grp", "batch"), "head"),
            P(("grp", "batch")),
            P(("grp", "batch"), "head", None),
            P(("grp", "batch"), "head"),
        ),
        out_specs=P(("grp", "batch"), "head", None),
        check_vma=False,
    )
```

profile of v0, /device:TPU:0, one launch (start us, length us, event | category | flops | bytes accessed | tf_op | source)
XLA Modules:
  0.0 87.3 jit_solution(7308756827463599597)
XLA Ops:
  0.0 0.9 %copy-done = bf16[16,32,128]{2,1,0:T(8,128)(2,1)S(1)} copy-done((bf16[16,32,128]{2,1,0:T(8,128)(2,1)S(1)}, bf16[16,32,128]{2,1,0:T(8,128)(2,1)}, u32[]{:S(2)}) %copy-start) | copy-done | bytes 131096
  0.9 0.7 broadcast_in_dim.71
  1.6 0.1 lt.87
  1.7 0.1 compare_bitcast_fusion
  1.9 3.4 %fusion.17 = f32[64,2,1,128]{3,2,1,0:T(1,128)S(1)} fusion(bf16[64,2,128,128]{3,2,1,0:T(8,128)(2,1)} %bitcast.70, pred[64,2,128,1]{2,1,0,3:T(4,128)(4,1)S(1)} %compare_bitcast_fusion), kind=kOutput, calls=%fused_computation.25 | convolution fusion | flops 4194304 | bytes 4276224 | tf_op jit(solution)/shard_map/pjt,pjtd->pjd/dot_general | solution.py:78
  5.4 3.4 %fusion.19 = f32[64,2,1,128]{3,2,1,0:T(1,128)S(1)} fusion(bf16[64,2,128,128]{3,2,1,0:T(8,128)(2,1)} %bitcast.68, pred[64,2,128,1]{2,1,0,3:T(4,128)(4,1)S(1)} %compare_bitcast_fusion), kind=kOutput, calls=%fused_computation.27 | convolution fusion | flops 4194304 | bytes 4276224 | tf_op jit(solution)/shard_map/pjt,pjtd->pjd/dot_general | solution.py:72
  8.8 0.1 fusion.24
  8.9 15.1 %all_gather.20 = bf16[64,8,128]{2,0,1:T(8,128)(2,1)S(1)} all-gather(bf16[64,2,128]{2,0,1:T(8,128)(2,1)S(1)} %get-tuple-element.207), channel_id=1, replica_groups=mesh['grp'=2,'seq'=4,'head'=2,'batch'=2] {'seq'}, dimensions={1}, use_global_device_ids=true | all-gather | bytes 163840 | tf_op jit(solution)/shard_map/all_gather | solution.py:127
  24.0 0.2 fusion.22
  24.2 0.1 copy.61
  24.4 0.1 copy.62
  24.7 0.1 lt.97
  24.8 0.1 copy.65
  24.9 0.1 eq.15
  25.0 0.1 and_reduce_fusion
  25.1 0.1 copy.67
  25.2 0.1 broadcast_in_dim.76
  25.4 3.5 %fusion.38 = (f32[64,8]{1,0:T(8,128)S(1)}, f32[64,8,256]{2,1,0:T(8,128)S(1)}) fusion(bf16[64,8,128]{2,1,0:T(8,128)(2,1)S(1)} %bitcast.67, bf16[64,256,128]{2,1,0:T(8,128)(2,1)} %bitcast.69, pred[64,256]{1,0:T(8,128)(4,1)S(1)} %bitcast_and_fusion), kind=kOutput, calls=%fused_computation.66 | convolution fusion | flops 33947136 | bytes 4868096 | tf_op jit(solution)/shard_map/pgd,pnd->pgn/dot_general | solution.py:31
  29.0 11.9 %all-gather.3 = bf16[4,64,8]{1,2,0:T(8,128)(2,1)S(1)} all-gather(bf16[1,64,8]{1,2,0:T(8,128)(2,1)S(1)} %copy.68), channel_id=2, replica_groups=mesh['grp'=2,'seq'=4,'head'=2,'batch'=2] {'seq'}, dimensions={0}, use_global_device_ids=true | all-gather | bytes 5120 | tf_op jit(solution)/shard_map/all_gather | solution.py:12
  40.9 0.3 fusion.12
  41.2 11.9 %all-gather.4 = bf16[4,64,8]{1,2,0:T(8,128)(2,1)S(1)} all-gather(bf16[1,64,8]{1,2,0:T(8,128)(2,1)S(1)} %copy.69), channel_id=3, replica_groups=mesh['grp'=2,'seq'=4,'head'=2,'batch'=2] {'seq'}, dimensions={0}, use_global_device_ids=true | all-gather | bytes 5120 | tf_op jit(solution)/shard_map/all_gather | solution.py:12
  53.2 2.9 %convolution_convert_fusion = bf16[64,8,128]{2,1,0:T(8,128)(2,1)S(1)} fusion(bf16[64,256,128]{2,1,0:T(8,128)(2,1)} %bitcast.71, f32[64,8,256]{2,1,0:T(8,128)S(1)} %get-tuple-element.210, f32[64,8]{1,0:T(8,128)S(1)} %get-tuple-element.209, pred[64,256]{1,0:T(8,128)(4,1)S(1)} %bitcast_and_fusion), kind=kOutput, calls=%fused_computation.15 | convolution fusion | flops 34013184 | bytes 4868096 | tf_op jit(solution)/shard_map/pgn,pnd->pgd/dot_general | solution.py:38
  56.1 15.0 %all-gather.2 = bf16[256,8,128]{2,1,0:T(8,128)(2,1)S(1)} all-gather(bf16[64,8,128]{2,1,0:T(8,128)(2,1)S(1)} %convolution_convert_fusion), channel_id=4, replica_groups=mesh['grp'=2,'seq'=4,'head'=2,'batch'=2] {'seq'}, dimensions={0}, use_global_device_ids=true | all-gather | bytes 655360 | tf_op jit(solution)/shard_map/all_gather | solution.py:12
  71.1 1.5 %while.19 = (s32[]{:T(128)}, f32[64,8]{0,1:T(8,128)S(1)}, f32[64,8]{0,1:T(8,128)S(1)}, f32[64,8,128]{2,1,0:T(8,128)S(1)}, bf16[4,64,8]{1,2,0:T(8,128)(2,1)S(1)},...) while((s32[]{:T(128)}, f32[64,8]{0,1:T(8,128)S(1)}, ...), condition=%wide.region_6.7_spmd, body=%wide.region_5.6_spmd.sunk | while | flops 266245 | bytes 682135 | solution.py:24
  71.2 0.1 copy.88
  71.3 0.3 fusion.49
  71.7 0.1 copy.88
  71.8 0.3 fusion.49
  72.2 0.1 copy.88
  72.3 0.3 fusion.49
  72.6 13.3 %all_gather.21 = bf16[64,8,128]{2,0,1:T(8,128)(2,1)S(1)} all-gather(bf16[64,2,128]{2,0,1:T(8,128)(2,1)S(1)} %get-tuple-element.206), channel_id=1, replica_groups=mesh['grp'=2,'seq'=4,'head'=2,'batch'=2] {'seq'}, dimensions={1}, use_global_device_ids=true | all-gather | bytes 163840 | tf_op jit(solution)/shard_map/all_gather | solution.py:128
  86.3 1.0 %fusion.7 = bf16[64,8,128]{2,1,0:T(8,128)(2,1)} fusion(bf16[64,8,8]{2,1,0:T(8,128)(2,1)S(1)} %copy.62, f32[64,8,128]{2,1,0:T(8,128)S(1)} %get-tuple-element.182, bf16[64,8,128]{2,0,1:T(8,128)(2,1)S(1)} %all_gather.21, f32[64,8]{1,0:T(8,128)S(1)} %copy.70, f32[64,8]{1,0:T(8,128)S(1)} %mul.134, f32[64,8]{1,0:T(8,128)S(1)} %copy.64, f32[64,8]{1,0:T(8,128)S(1)} %mul.125), kind=kOutput, calls=%fused_computation.14 | convolution fusion | flops 1441792 | bytes 540672 | tf_op jit(solution)/shard_map/pgn,pnd->pgd/dot_general | solution.py:38
  (35 shorter events, 1.2 us)
Async XLA Ops:
  0.0 0.9 %copy-start = (bf16[16,32,128]{2,1,0:T(8,128)(2,1)S(1)}, bf16[16,32,128]{2,1,0:T(8,128)(2,1)}, u32[]{:S(2)}) copy-start(bf16[16,32,128]{2,1,0:T(8,128)(2,1)} %param.9) | copy-start | bytes 393220
  1.9 22.7 %copy-start.3 = (s32[16,4]{0,1:T(4,128)S(1)}, s32[16,4]{0,1:T(4,128)}, u32[]{:S(2)}) copy-start(s32[16,4]{0,1:T(4,128)} %param.15) | copy-start | bytes 772
  1.9 22.9 %copy-start.2 = (s32[16,4,2]{0,2,1:T(2,128)S(1)}, s32[16,4,2]{0,2,1:T(2,128)}, u32[]{:S(2)}) copy-start(s32[16,4,2]{0,2,1:T(2,128)} %param.14) | copy-start | bytes 1540
  53.2 32.9 %copy-start.1 = (f32[2,16,32]{2,1,0:T(8,128)S(1)}, f32[2,16,32]{2,1,0:T(8,128)}, u32[]{:S(2)}) copy-start(f32[2,16,32]{2,1,0:T(8,128)} %param.12) | copy-start | bytes 12292
where the time goes:
time: 87.6 us; the launch traced here: 87.3 us
  blocking collectives  67.3 us (77%)
  matrix products  14.3 us (16%)
  local copies, waits for them, and re-layouts  3.58 us (4%)
  other arithmetic  1.83 us (2%)
    all_gather x3, blocking collectives, combined_all(): lax.all_gather(a.astype(kind), axis)  38.9 us
    all_gather x1, blocking collectives, on_device(): lax.all_gather(pooled_keys, 'seq', axis=1, tiled=True)  15.1 us
    all_gather x1, blocking collectives, on_device(): lax.all_gather(pooled_values, 'seq', axis=1, tiled=True)  13.3 us
    dot_general x2, matrix products, softmax_terms(): jnp.einsum('pgn,pnd->pgd', weights.astype(jnp.bfloat16), value_rows, pref...  3.93 us
    dot_general x2, matrix products, softmax_terms(): jnp.einsum('pgd,pnd->pgn', query_rows, key_rows, preferred_element_type=j...  3.65 us
    dot_general x1, matrix products, pool_blocks(): jnp.einsum('pjt,pjtd->pjd', token_ones, key_rows.reshape(pair_count, bloc...  3.39 us
    dot_general x1, matrix products, pool_blocks(): jnp.einsum('pjt,pjtd->pjd', token_ones, value_rows.reshape(pair_count, bl...  3.38 us

commit v1 on v0

--- a/solution.py
+++ b/solution.py
@@ -125,7 +125,9 @@
     token_mask = picked_tokens(live_mask, pair_chosen, pair_counts, first_block)
     all_keys, all_values = (
         lax.all_gather(pooled_keys, "seq", axis=1, tiled=True),
-        lax.all_gather(pooled_values, "seq", axis=1, tiled=True),
+        jnp.concatenate(
+            lax.all_to_all(jnp.stack([pooled_values] * lax.axis_size("seq")), "seq", 0, 0), axis=1
+        ),
     )
     all_starts = jnp.arange(all_keys.shape[1], dtype=jnp.int32) * BLOCK
     all_live = all_starts[None, :] < pair_lengths[:, None]

time: 87.6 us -> 75.9 us (0.87)
  blocking collectives: 67.3 us -> 53.3 us
  starting transfers between devices: 0 us -> 6.35 us
  matrix products: 14.3 us -> 10.3 us
    all_gather x1 -> x0, blocking collectives: 13.3 us -> none  [on_device(): lax.all_gather(pooled_values, 'seq', axis=1, tiled=True)]
    all_to_all x0 -> x1, starting transfers between devices: none -> 6.35 us  [on_device(): lax.all_to_all(jnp.stack([pooled_values] * lax.axis_size('seq')), 'seq',...]
    dot_general x2, matrix products: 3.93 us -> 1.72 us  [softmax_terms(): jnp.einsum('pgn,pnd->pgd', weights.astype(jnp.bfloat16), value_rows, pref...]
    dot_general x1, matrix products: 3.39 us -> 1.2 us  [pool_blocks(): jnp.einsum('pjt,pjtd->pjd', token_ones, key_rows.reshape(pair_count, bloc...]
    all_gather x1, blocking collectives: 15.1 us -> 13.3 us  [on_device(): lax.all_gather(pooled_keys, 'seq', axis=1, tiled=True)]
    all_gather x3, blocking collectives: 38.9 us -> 40 us  [combined_all(): lax.all_gather(a.astype(kind), axis)]
    unnamed x12 -> x16, local copies, waits for them, and re-layouts: 1.25 us -> 0.35 us
  transfers between devices with their start and end apart: 0 -> 1, of which waited for: 0 -> 0; matrix products, arithmetic and copies ran while one was open for 0% -> 10% of each run, Pallas kernels for 0% -> 0%
where the time goes in v1:
time: 75.9 us; the launch traced here: 75.6 us
  blocking collectives  53.3 us (70%)
  matrix products  10.3 us (14%)
  starting transfers between devices  6.35 us (8%)
  local copies, waits for them, and re-layouts  3.57 us (5%)
  other arithmetic  1.83 us (2%)
    all_gather x3, blocking collectives, combined_all(): lax.all_gather(a.astype(kind), axis)  40 us
    all_gather x1, blocking collectives, on_device(): lax.all_gather(pooled_keys, 'seq', axis=1, tiled=True)  13.3 us
    all_to_all x1, starting transfers between devices, on_device(): lax.all_to_all(jnp.stack([pooled_values] * lax.axis_size('seq')), 'seq',...  6.35 us
    dot_general x2, matrix products, softmax_terms(): jnp.einsum('pgd,pnd->pgn', query_rows, key_rows, preferred_element_type=j...  3.8 us
    dot_general x1, matrix products, pool_blocks(): jnp.einsum('pjt,pjtd->pjd', token_ones, value_rows.reshape(pair_count, bl...  3.53 us
    dot_general x2, matrix products, softmax_terms(): jnp.einsum('pgn,pnd->pgd', weights.astype(jnp.bfloat16), value_rows, pref...  1.72 us
  transfers between devices with their start and end apart: 1, of which 0 were waited for; matrix products, arithmetic and copies ran while one was open for 10% of the time, Pallas kernels for 0%

profile of v1, /device:TPU:0, one launch (start us, length us, event | category | flops | bytes accessed | tf_op | source)
XLA Modules:
  0.0 75.6 jit_solution(15831346053594128486)
XLA Ops:
  0.0 0.8 %broadcast_in_dim.71 = s32[16,4]{1,0:T(8,128)S(1)} broadcast(s32[16]{0:T(128)} %param.13), dimensions={0} | broadcast | bytes 320 | tf_op jit(solution)/shard_map/broadcast_in_dim | solution.py:116
  0.8 0.1 lt.87
  0.9 0.1 compare_bitcast_fusion
  1.1 3.5 %fusion.17 = f32[64,2,1,128]{3,2,1,0:T(1,128)S(1)} fusion(bf16[64,2,128,128]{3,2,1,0:T(8,128)(2,1)} %bitcast.73, pred[64,2,128,1]{2,1,0,3:T(4,128)(4,1)S(1)} %compare_bitcast_fusion), kind=kOutput, calls=%fused_computation.25 | convolution fusion | flops 4194304 | bytes 4276224 | tf_op jit(solution)/shard_map/pjt,pjtd->pjd/dot_general | solution.py:78
  4.6 1.2 %fusion.19 = f32[64,2,1,128]{3,2,1,0:T(1,128)S(1)} fusion(bf16[64,2,128,128]{3,2,1,0:T(8,128)(2,1)S(1)} %bitcast.72, pred[64,2,128,1]{2,1,0,3:T(4,128)(4,1)S(1)} %compare_bitcast_fusion), kind=kOutput, calls=%fused_computation.27 | convolution fusion | flops 4194304 | bytes 4276224 | tf_op jit(solution)/shard_map/pjt,pjtd->pjd/dot_general | solution.py:72
  5.9 0.1 fusion.23
  6.0 0.7 stack.2
  6.8 6.3 %all-to-all-start = ((bf16[4,64,2,128]{3,2,1,0:T(2,128)(2,1)}), bf16[4,64,2,128]{3,2,1,0:T(2,128)(2,1)S(1)}, u32[]{:S(2)}, u32[]{:S(2)}) async-start(bf16[4,64,2,128]{3,2,1,0:T(2,128)(2,1)} %stack.2), calls=%async_computation | async-start | bytes 262144 | tf_op jit(solution)/shard_map/all_to_all | solution.py:129
  13.1 0.1 copy.69
  13.2 0.1 eq.15
  13.4 0.1 lt.97
  13.6 0.1 copy.71
  13.7 0.1 broadcast_in_dim.76
  13.9 3.6 %fusion.37 = (f32[64,8]{1,0:T(8,128)S(1)}, f32[64,8,256]{2,1,0:T(8,128)S(1)}) fusion(bf16[64,8,128]{2,1,0:T(8,128)(2,1)S(1)} %bitcast.70, bf16[64,256,128]{2,1,0:T(8,128)(2,1)} %bitcast.71, pred[64,256]{1,0:T(8,128)(4,1)S(1)} %bitcast_and_fusion), kind=kOutput, calls=%fused_computation.65 | convolution fusion | flops 33947136 | bytes 4868096 | tf_op jit(solution)/shard_map/pgd,pnd->pgn/dot_general | solution.py:31
  17.6 0.3 fusion.12
  17.8 0.7 convolution_convert_fusion
  18.6 15.8 %all-gather.2 = bf16[256,8,128]{2,1,0:T(8,128)(2,1)S(1)} all-gather(bf16[64,8,128]{2,1,0:T(8,128)(2,1)S(1)} %convolution_convert_fusion), channel_id=4, replica_groups=mesh['grp'=2,'seq'=4,'head'=2,'batch'=2] {'seq'}, dimensions={0}, use_global_device_ids=true | all-gather | bytes 655360 | tf_op jit(solution)/shard_map/all_gather | solution.py:12
  34.5 12.2 %all-gather.4 = bf16[4,64,8]{1,2,0:T(8,128)(2,1)S(1)} all-gather(bf16[1,64,8]{1,2,0:T(8,128)(2,1)S(1)} %copy.73), channel_id=3, replica_groups=mesh['grp'=2,'seq'=4,'head'=2,'batch'=2] {'seq'}, dimensions={0}, use_global_device_ids=true | all-gather | bytes 5120 | tf_op jit(solution)/shard_map/all_gather | solution.py:12
  46.8 12.0 %all-gather.3 = bf16[4,64,8]{1,2,0:T(8,128)(2,1)S(1)} all-gather(bf16[1,64,8]{1,2,0:T(8,128)(2,1)S(1)} %copy.72), channel_id=2, replica_groups=mesh['grp'=2,'seq'=4,'head'=2,'batch'=2] {'seq'}, dimensions={0}, use_global_device_ids=true | all-gather | bytes 5120 | tf_op jit(solution)/shard_map/all_gather | solution.py:12
  58.7 1.5 %while.19 = (s32[]{:T(128)}, f32[64,8]{0,1:T(8,128)S(1)}, f32[64,8]{0,1:T(8,128)S(1)}, f32[64,8,128]{2,1,0:T(8,128)S(1)}, bf16[4,64,8]{1,2,0:T(8,128)(2,1)S(1)},...) while((s32[]{:T(128)}, f32[64,8]{0,1:T(8,128)S(1)}, ...), condition=%wide.region_6.7_spmd, body=%wide.region_5.6_spmd.sunk | while | flops 266245 | bytes 682135 | solution.py:24
  58.8 0.1 copy.90
  58.9 0.3 fusion.49
  59.2 0.1 copy.90
  59.4 0.3 fusion.49
  59.7 0.1 copy.90
  59.9 0.3 fusion.49
  60.3 13.3 %all_gather.17 = bf16[64,8,128]{2,0,1:T(8,128)(2,1)S(1)} all-gather(bf16[64,2,128]{2,0,1:T(8,128)(2,1)S(1)} %get-tuple-element.207), channel_id=1, replica_groups=mesh['grp'=2,'seq'=4,'head'=2,'batch'=2] {'seq'}, dimensions={1}, use_global_device_ids=true | all-gather | bytes 163840 | tf_op jit(solution)/shard_map/all_gather | solution.py:127
  73.6 0.2 fusion.21
  73.8 0.1 copy.64
  74.1 0.1 copy.67
  74.5 0.1 copy.66
  74.6 1.0 %fusion.7 = bf16[64,8,128]{2,1,0:T(8,128)(2,1)} fusion(bf16[64,8,8]{2,1,0:T(8,128)(2,1)S(1)} %copy.67, bf16[64,8,128]{2,1,0:T(8,128)(2,1)S(1)} %bitcast.78, f32[64,8,128]{2,1,0:T(8,128)S(1)} %get-tuple-element.182, f32[64,8]{1,0:T(8,128)S(1)} %copy.74, f32[64,8]{1,0:T(8,128)S(1)} %mul.134, f32[64,8]{1,0:T(8,128)S(1)} %copy.68, f32[64,8]{1,0:T(8,128)S(1)} %mul.125), kind=kOutput, calls=%fused_computation.14 | convolution fusion | flops 1441792 | bytes 540672 | tf_op jit(solution)/shard_map/pgn,pnd->pgd/dot_general | solution.py:38
  (43 shorter events, 1.4 us)
Async XLA Ops:
  0.0 13.9 %copy-start = (bf16[16,32,128]{2,1,0:T(8,128)(2,1)S(1)}, bf16[16,32,128]{2,1,0:T(8,128)(2,1)}, u32[]{:S(2)}) copy-start(bf16[16,32,128]{2,1,0:T(8,128)(2,1)} %param.9) | copy-start | bytes 393220
  0.9 3.7 %copy-start.1 = (bf16[16,4,256,128]{3,2,1,0:T(8,128)(2,1)S(1)}, bf16[16,4,256,128]{3,2,1,0:T(8,128)(2,1)}, u32[]{:S(2)}) copy-start(bf16[16,4,256,128]{3,2,1,0:T(8,128)(2,1)} %param.10) | copy-start | bytes 12582916
  1.0 12.1 %copy-start.4 = (s32[16,4,2]{0,2,1:T(2,128)S(1)}, s32[16,4,2]{0,2,1:T(2,128)}, u32[]{:S(2)}) copy-start(s32[16,4,2]{0,2,1:T(2,128)} %param.14) | copy-start | bytes 1540
  1.0 12.3 %copy-start.5 = (s32[16,4]{0,1:T(4,128)S(1)}, s32[16,4]{0,1:T(4,128)}, u32[]{:S(2)}) copy-start(s32[16,4]{0,1:T(4,128)} %param.15) | copy-start | bytes 772
  6.8 67.7 %all-to-all-start = ((bf16[4,64,2,128]{3,2,1,0:T(2,128)(2,1)}), bf16[4,64,2,128]{3,2,1,0:T(2,128)(2,1)S(1)}, u32[]{:S(2)}, u32[]{:S(2)}) async-start(bf16[4,64,2,128]{3,2,1,0:T(2,128)(2,1)} %stack.2), calls=%async_computation | async-start | bytes 262144 | tf_op jit(solution)/shard_map/all_to_all | solution.py:129
  13.7 4.1 %copy-start.2 = (bf16[16,4,256,128]{3,2,1,0:T(8,128)(2,1)S(1)}, bf16[16,4,256,128]{3,2,1,0:T(8,128)(2,1)}, u32[]{:S(2)}) copy-start(bf16[16,4,256,128]{3,2,1,0:T(8,128)(2,1)} %param.11) | copy-start | bytes 12582916
  18.6 55.8 %copy-start.3 = (f32[2,16,32]{2,1,0:T(8,128)S(1)}, f32[2,16,32]{2,1,0:T(8,128)}, u32[]{:S(2)}) copy-start(f32[2,16,32]{2,1,0:T(8,128)} %param.12) | copy-start | bytes 12292
